TPU v7x, 32 devices: a whole 2x2x4 slice. The times are simulated.
32 devices in a mesh: grp: 2 (over core), tile: 16 (over z, y, x).
Axes of the slice: x: 2, y: 2, z: 4, core: 2. Of those that a mesh axis runs over, the one named last changes fastest.
Arguments:
- source_points: float32 [2, 3, 524288], P('grp', None, 'tile'), may hold values from -6 to 6
- intersection: int32 [2, 2048, 1], P('grp', 'tile'), may hold values from 0 to 15; in each aligned block of 128 rows (0 to 127, 128 to 255, ..., all dimensions but the last counted through in order) at most 16 rows name the same one
- target_scan: int32 [2, 2048], P('grp', 'tile'), may hold values from 0 to 63
- matches: int32 [2, 524288], P('grp', 'tile'), may hold values from 0 to 511
- target_points: float32 [3, 524288], P(None, 'tile'), may hold values from -6 to 6
- target_normals: float32 [3, 524288], P(None, 'tile'), may hold values from -4 to 4
Outputs:
- pose_step: float32 [6, 1024], P(None, 'tile')
Inputs may be any that keep to these rules, and one draw needn't show every extreme that they name: `intersection`: within the blocks of one device (each aligned run of 128 rows), no index is named more than 16 times, a bound that some block reaches.
All inputs are finite; a program needn't handle non-finite values.
Results may differ from a plain program's by a relative error of at most 0.0003.
Values sent between devices are 32-bit elements; how exact they have to be, the bound alone decides.
A program may use at most 64 MiB of HBM per device.

v0:
```python
import math

import jax
import jax.numpy as jnp
from jax import lax
from jax.sharding import PartitionSpec as P

SCANS_DEV = 64
TARGET_PTS = 512


DAMPING = 0.1
PRECISE = lax.Precision.HIGHEST


def cross_rows(first_vec, second_vec):
    return jnp.stack(
        [
            first_vec[1] * second_vec[2] - first_vec[2] * second_vec[1],
            first_vec[2] * second_vec[0] - first_vec[0] * second_vec[2],
            first_vec[0] * second_vec[1] - first_vec[1] * second_vec[0],
        ]
    )


def pair_terms(source, target, normal, usable):
    jacobian = (
        jnp.concatenate(
            [cross_rows(source, normal), normal, -cross_rows(target, normal), -normal], axis=0
        )
        * usable[None]
    )
    misfit = jnp.sum(normal * (source - target), axis=0) * usable
    normal_blocks = jnp.einsum("anks,bnks->abnk", jacobian, jacobian, precision=PRECISE)
    gradient = jnp.einsum("anks,nks->ank", jacobian, misfit, precision=PRECISE)
    layout = jacobian.shape[1:3]
    own_terms = jnp.concatenate(
        [normal_blocks[:6, :6].reshape((36,) + layout), gradient[:6]], axis=0
    )
    theirs = jnp.concatenate([normal_blocks[6:, 6:].reshape((36,) + layout), gradient[6:]], axis=0)
    return (own_terms, theirs)


def solve_poses(scan_totals):
    entries = [[scan_totals[6 * row_at + col_at] for col_at in range(6)] for row_at in range(6)]
    traced = entries[0][0]
    for step_at in range(1, 6):
        traced = traced + entries[step_at][step_at]
    shift_by = DAMPING * traced / 6.0
    for step_at in range(6):
        entries[step_at][step_at] = entries[step_at][step_at] + shift_by
    values = [-scan_totals[36 + row_at] for row_at in range(6)]
    for pivot_at in range(6):
        for row_at in range(pivot_at + 1, 6):
            factor = entries[row_at][pivot_at] / entries[pivot_at][pivot_at]
            for col_at in range(pivot_at, 6):
                entries[row_at][col_at] = (
                    entries[row_at][col_at] - factor * entries[pivot_at][col_at]
                )
            values[row_at] = values[row_at] - factor * values[pivot_at]
    result = [None] * 6
    for row_at in range(5, -1, -1):
        running = values[row_at]
        for col_at in range(row_at + 1, 6):
            running = running - entries[row_at][col_at] * result[col_at]
        result[row_at] = running / entries[row_at][row_at]
    return jnp.stack(result)


def body(source_points, intersection, target_scan, matches, target_points, target_normals):
    tile_count = lax.axis_size("tile")
    blocks = intersection.shape[1]
    capacity = 2 * blocks // tile_count
    slot_count = tile_count * capacity
    points = source_points.shape[2] // blocks
    per_scan = blocks // SCANS_DEV
    destin = intersection[0, :, 0]
    block_range = jnp.arange(blocks, dtype=jnp.int32)
    onehot_dest = (destin[:, None] == jnp.arange(tile_count, dtype=jnp.int32)[None, :]).astype(
        jnp.float32
    )
    lower = (block_range[:, None] >= block_range[None, :]).astype(jnp.float32)
    running = jnp.dot(lower, onehot_dest, precision=PRECISE)
    ranked = jnp.sum(running * onehot_dest, axis=1).astype(jnp.int32) - 1
    slot_of = destin * capacity + ranked
    placing = (slot_of[None, :] == jnp.arange(slot_count, dtype=jnp.int32)[:, None]).astype(
        jnp.float32
    )
    filled = jnp.sum(placing, axis=1) > 0.5
    safe_block = jnp.dot(placing, block_range.astype(jnp.float32), precision=PRECISE).astype(
        jnp.int32
    )
    shaped = (tile_count, capacity, points)
    coords = source_points[0].reshape(3, blocks, points)
    packed = jnp.einsum("sb,cbk->csk", placing, coords, precision=PRECISE).reshape((3,) + shaped)
    wanted = (target_scan[0][:, None] * TARGET_PTS + matches[0].reshape(blocks, points)).astype(
        jnp.float32
    )
    placed = jnp.dot(placing, wanted, precision=PRECISE).astype(jnp.int32)
    request = jnp.where(filled[:, None], placed, -1).reshape((1,) + shaped)
    tables = jnp.concatenate([target_points, target_normals], axis=0).reshape(
        6, SCANS_DEV, TARGET_PTS
    )
    tables = jnp.transpose(tables, (1, 0, 2)).reshape(SCANS_DEV, 6 * TARGET_PTS)
    scan_range = jnp.arange(SCANS_DEV, dtype=jnp.int32)
    column_range = jnp.arange(TARGET_PTS, dtype=jnp.int32)
    outgoing = jnp.concatenate([packed, request.astype(jnp.float32)], axis=0)
    incoming = lax.all_to_all(outgoing, "tile", split_axis=1, concat_axis=1, tiled=True)
    target_index = incoming[3:].astype(jnp.int32)
    lookup_target_index = target_index[0]
    outer = lookup_target_index.shape[:-1]
    width = lookup_target_index.shape[-1]
    items = math.prod(outer)
    flat = jnp.maximum(lookup_target_index, 0).reshape(items, width)
    item_scan = flat[:, 0] // TARGET_PTS
    within = flat % TARGET_PTS
    scan_pick = (item_scan[:, None] == scan_range[None, :]).astype(jnp.float32)
    block_tables = jnp.dot(scan_pick, tables, precision=PRECISE).reshape(items, 6, TARGET_PTS)
    group = math.gcd(items, 16)

    def select(pair):
        table_part, column_part = pair
        chooser = (column_part[:, None, :] == column_range[None, :, None]).astype(jnp.float32)
        return jnp.einsum("icj,ijk->ick", table_part, chooser, precision=PRECISE)

    picked = lax.map(
        select,
        (
            block_tables.reshape(items // group, group, 6, TARGET_PTS),
            within.reshape(items // group, group, width),
        ),
    )
    picked = jnp.transpose(picked.reshape(items, 6, width), (1, 0, 2)).reshape(
        (6,) + outer + (width,)
    )
    nearest = picked[:3]
    facing = picked[3:]
    usable = (target_index[0] >= 0).astype(jnp.float32)
    mine, far_terms = pair_terms(incoming[:3], nearest, facing, usable)
    returned = lax.all_to_all(mine, "tile", split_axis=1, concat_axis=1, tiled=True)
    leading = target_index[:, :, :, 0]
    owner_scan = jnp.where(leading >= 0, leading // TARGET_PTS, -1)
    source_scan = jnp.where(filled, safe_block // per_scan, -1)
    src_onehot = (source_scan[None, :] == scan_range[:, None]).astype(jnp.float32)
    tgt_onehot = (owner_scan.reshape(slot_count)[None, :] == scan_range[:, None]).astype(
        jnp.float32
    )
    local_sums = jnp.dot(returned.reshape(42, slot_count), src_onehot.T, precision=PRECISE)
    local_sums = local_sums + jnp.dot(
        far_terms.reshape(42, slot_count), tgt_onehot.T, precision=PRECISE
    )
    totals = lax.psum(local_sums, "grp")
    return solve_poses(totals)


def solution(mesh):
    in_specs = (
        P("grp", None, "tile"),
        P("grp", "tile", None),
        P("grp", "tile"),
        P("grp", "tile"),
        P(None, "tile"),
        P(None, "tile"),
    )
    out_specs = P(None, "tile")
    return jax.shard_map(body, mesh=mesh, in_specs=in_specs, out_specs=out_specs, check_vma=False)
```

profile of v0, /device:TPU:0, one launch (start us, length us, event | category | flops | bytes accessed | tf_op | source)
XLA Modules:
  0.0 147.4 jit_solution(17331304386599116131)
XLA Ops:
  2.5 1.9 %reduce.10 = s32[32768]{0:T(1024)S(1)} reduce(s32[1,32768]{1,0:T(1,128)} %param.11, s32[]{:T(128)} %broadcast.193), dimensions={0}, to_apply=%param.11.reduce_sub_computation.3 | reduce | bytes 262148 | tf_op args[3]
  5.1 2.1 %reduce = f32[3,32768]{1,0:T(4,128)S(1)} reduce(f32[1,3,32768]{2,0,1:T(1,128)} %param.8, f32[]{:T(128)} %constant.83), dimensions={0}, to_apply=%param.8.reduce_sub_computation | reduce | bytes 786436 | tf_op args[0]
  8.1 1.1 pad_maximum_fusion
  9.2 8.3 %all-to-all-start = ((f32[4,16,16,256]{3,2,0,1:T(8,128)}), f32[4,16,16,256]{3,2,0,1:T(8,128)S(1)}, u32[]{:S(2)}, u32[]{:S(2)}) async-start(f32[4,16,16,256]{3,2,0,1:T(8,128)} %pad_maximum_fusion), calls=%async_computation | async-start | bytes 2097152 | tf_op jit(solution)/shard_map/all_to_all | solution.py:108
  17.5 2.2 %pad_maximum_fusion.1 = f32[6,32768]{1,0:T(8,128)} fusion(f32[3,32768]{1,0:T(4,128)S(1)} %copy-done.2, f32[3,32768]{1,0:T(4,128)} %param.12), kind=kLoop, calls=%fused_computation.22 | loop fusion | flops 196608 | bytes 1572864 | tf_op jit(solution)/shard_map/concatenate | solution.py:101
  19.8 22.1 %all-to-all-done = f32[4,16,16,256]{3,2,0,1:T(8,128)S(1)} async-done(((f32[4,16,16,256]{3,2,0,1:T(8,128)}), f32[4,16,16,256]{3,2,0,1:T(8,128)S(1)}, u32[]{:S(2)}, u32[]{:S(2)}) %all-to-all-start) | async-done | bytes 1048608 | tf_op jit(solution)/shard_map/all_to_all | solution.py:108
  42.1 4.7 %fusion.15 = f32[16,16,6,512]{3,1,2,0:T(8,128)} fusion(s32[16,16]{1,0:T(8,128)S(1)} %eq.106, f32[8,8,6,512]{3,2,1,0:T(8,128)} %bitcast.126), kind=kOutput, calls=%fused_computation.24 | convolution fusion | flops 603996160 | bytes 3933184 | tf_op jit(solution)/shard_map/dot_general | solution.py:118
  47.0 60.6 %while.11 = (s32[]{:T(128)}, f32[16,16,6,256]{3,1,0,2:T(8,128)S(1)}, f32[16,16,6,512]{3,1,2,0:T(8,128)}, s32[16,16,256]{2,1,0:T(8,128)S(1)}, s32[]{:T(128)}) while((s32[]{:T(128)}, f32[16,16,6,256]{3,1,0,2:T(8,128)S(1)}, f32[16,16,6,512]{3,1,2,0:T(8,128)}, s32[16,16,256]{2,1,0:T(8,128)S(1)}, s32[]{:T(128)}) %tuple.70), condition=%wide.region_3.4_spmd.clone, body=%wide.region_2.3_spmd.clone.sunk | while | flops 153092096 | bytes 966729 | solution.py:126
  47.0 0.9 constant_dynamic-slice_fusion.2
  48.0 2.7 %fusion.107 = f32[1,16,6,256]{3,2,1,0:T(8,128)S(1)} fusion(s32[16,256]{1,0:T(8,128)S(1)} %dynamic-slice_bitcast_fusion.2, f32[1,16,6,512]{3,1,2,0:T(8,128)S(1)} %constant_dynamic-slice_fusion.2), kind=kOutput, calls=%fused_computation.4.clone.1 | convolution fusion | flops 153092096 | bytes 311296 | tf_op jit(solution)/shard_map/while/body/eval_jaxpr/icj,ijk->ick/dot_general | solution.py:124
  50.8 0.9 constant_dynamic-slice_fusion.2
  51.7 2.7 %fusion.107 = f32[1,16,6,256]{3,2,1,0:T(8,128)S(1)} fusion(s32[16,256]{1,0:T(8,128)S(1)} %dynamic-slice_bitcast_fusion.2, f32[1,16,6,512]{3,1,2,0:T(8,128)S(1)} %constant_dynamic-slice_fusion.2), kind=kOutput, calls=%fused_computation.4.clone.1 | convolution fusion | flops 153092096 | bytes 311296 | tf_op jit(solution)/shard_map/while/body/eval_jaxpr/icj,ijk->ick/dot_general | solution.py:124
  54.5 0.9 constant_dynamic-slice_fusion.2
  55.5 2.7 %fusion.107 = f32[1,16,6,256]{3,2,1,0:T(8,128)S(1)} fusion(s32[16,256]{1,0:T(8,128)S(1)} %dynamic-slice_bitcast_fusion.2, f32[1,16,6,512]{3,1,2,0:T(8,128)S(1)} %constant_dynamic-slice_fusion.2), kind=kOutput, calls=%fused_computation.4.clone.1 | convolution fusion | flops 153092096 | bytes 311296 | tf_op jit(solution)/shard_map/while/body/eval_jaxpr/icj,ijk->ick/dot_general | solution.py:124
  58.3 0.9 constant_dynamic-slice_fusion.2
  59.3 2.7 %fusion.107 = f32[1,16,6,256]{3,2,1,0:T(8,128)S(1)} fusion(s32[16,256]{1,0:T(8,128)S(1)} %dynamic-slice_bitcast_fusion.2, f32[1,16,6,512]{3,1,2,0:T(8,128)S(1)} %constant_dynamic-slice_fusion.2), kind=kOutput, calls=%fused_computation.4.clone.1 | convolution fusion | flops 153092096 | bytes 311296 | tf_op jit(solution)/shard_map/while/body/eval_jaxpr/icj,ijk->ick/dot_general | solution.py:124
  62.1 0.9 constant_dynamic-slice_fusion.2
  63.1 2.7 %fusion.107 = f32[1,16,6,256]{3,2,1,0:T(8,128)S(1)} fusion(s32[16,256]{1,0:T(8,128)S(1)} %dynamic-slice_bitcast_fusion.2, f32[1,16,6,512]{3,1,2,0:T(8,128)S(1)} %constant_dynamic-slice_fusion.2), kind=kOutput, calls=%fused_computation.4.clone.1 | convolution fusion | flops 153092096 | bytes 311296 | tf_op jit(solution)/shard_map/while/body/eval_jaxpr/icj,ijk->ick/dot_general | solution.py:124
  65.9 0.9 constant_dynamic-slice_fusion.2
  66.8 2.7 %fusion.107 = f32[1,16,6,256]{3,2,1,0:T(8,128)S(1)} fusion(s32[16,256]{1,0:T(8,128)S(1)} %dynamic-slice_bitcast_fusion.2, f32[1,16,6,512]{3,1,2,0:T(8,128)S(1)} %constant_dynamic-slice_fusion.2), kind=kOutput, calls=%fused_computation.4.clone.1 | convolution fusion | flops 153092096 | bytes 311296 | tf_op jit(solution)/shard_map/while/body/eval_jaxpr/icj,ijk->ick/dot_general | solution.py:124
  69.6 0.9 constant_dynamic-slice_fusion.2
  70.6 2.7 %fusion.107 = f32[1,16,6,256]{3,2,1,0:T(8,128)S(1)} fusion(s32[16,256]{1,0:T(8,128)S(1)} %dynamic-slice_bitcast_fusion.2, f32[1,16,6,512]{3,1,2,0:T(8,128)S(1)} %constant_dynamic-slice_fusion.2), kind=kOutput, calls=%fused_computation.4.clone.1 | convolution fusion | flops 153092096 | bytes 311296 | tf_op jit(solution)/shard_map/while/body/eval_jaxpr/icj,ijk->ick/dot_general | solution.py:124
  73.4 0.9 constant_dynamic-slice_fusion.2
  74.4 2.7 %fusion.107 = f32[1,16,6,256]{3,2,1,0:T(8,128)S(1)} fusion(s32[16,256]{1,0:T(8,128)S(1)} %dynamic-slice_bitcast_fusion.2, f32[1,16,6,512]{3,1,2,0:T(8,128)S(1)} %constant_dynamic-slice_fusion.2), kind=kOutput, calls=%fused_computation.4.clone.1 | convolution fusion | flops 153092096 | bytes 311296 | tf_op jit(solution)/shard_map/while/body/eval_jaxpr/icj,ijk->ick/dot_general | solution.py:124
  77.2 0.9 constant_dynamic-slice_fusion.2
  78.2 2.7 %fusion.107 = f32[1,16,6,256]{3,2,1,0:T(8,128)S(1)} fusion(s32[16,256]{1,0:T(8,128)S(1)} %dynamic-slice_bitcast_fusion.2, f32[1,16,6,512]{3,1,2,0:T(8,128)S(1)} %constant_dynamic-slice_fusion.2), kind=kOutput, calls=%fused_computation.4.clone.1 | convolution fusion | flops 153092096 | bytes 311296 | tf_op jit(solution)/shard_map/while/body/eval_jaxpr/icj,ijk->ick/dot_general | solution.py:124
  81.0 0.9 constant_dynamic-slice_fusion.2
  81.9 2.7 %fusion.107 = f32[1,16,6,256]{3,2,1,0:T(8,128)S(1)} fusion(s32[16,256]{1,0:T(8,128)S(1)} %dynamic-slice_bitcast_fusion.2, f32[1,16,6,512]{3,1,2,0:T(8,128)S(1)} %constant_dynamic-slice_fusion.2), kind=kOutput, calls=%fused_computation.4.clone.1 | convolution fusion | flops 153092096 | bytes 311296 | tf_op jit(solution)/shard_map/while/body/eval_jaxpr/icj,ijk->ick/dot_general | solution.py:124
  84.7 0.9 constant_dynamic-slice_fusion.2
  85.7 2.7 %fusion.107 = f32[1,16,6,256]{3,2,1,0:T(8,128)S(1)} fusion(s32[16,256]{1,0:T(8,128)S(1)} %dynamic-slice_bitcast_fusion.2, f32[1,16,6,512]{3,1,2,0:T(8,128)S(1)} %constant_dynamic-slice_fusion.2), kind=kOutput, calls=%fused_computation.4.clone.1 | convolution fusion | flops 153092096 | bytes 311296 | tf_op jit(solution)/shard_map/while/body/eval_jaxpr/icj,ijk->ick/dot_general | solution.py:124
  88.5 0.9 constant_dynamic-slice_fusion.2
  89.5 2.7 %fusion.107 = f32[1,16,6,256]{3,2,1,0:T(8,128)S(1)} fusion(s32[16,256]{1,0:T(8,128)S(1)} %dynamic-slice_bitcast_fusion.2, f32[1,16,6,512]{3,1,2,0:T(8,128)S(1)} %constant_dynamic-slice_fusion.2), kind=kOutput, calls=%fused_computation.4.clone.1 | convolution fusion | flops 153092096 | bytes 311296 | tf_op jit(solution)/shard_map/while/body/eval_jaxpr/icj,ijk->ick/dot_general | solution.py:124
  92.3 0.9 constant_dynamic-slice_fusion.2
  93.3 2.7 %fusion.107 = f32[1,16,6,256]{3,2,1,0:T(8,128)S(1)} fusion(s32[16,256]{1,0:T(8,128)S(1)} %dynamic-slice_bitcast_fusion.2, f32[1,16,6,512]{3,1,2,0:T(8,128)S(1)} %constant_dynamic-slice_fusion.2), kind=kOutput, calls=%fused_computation.4.clone.1 | convolution fusion | flops 153092096 | bytes 311296 | tf_op jit(solution)/shard_map/while/body/eval_jaxpr/icj,ijk->ick/dot_general | solution.py:124
  96.1 0.9 constant_dynamic-slice_fusion.2
  97.0 2.7 %fusion.107 = f32[1,16,6,256]{3,2,1,0:T(8,128)S(1)} fusion(s32[16,256]{1,0:T(8,128)S(1)} %dynamic-slice_bitcast_fusion.2, f32[1,16,6,512]{3,1,2,0:T(8,128)S(1)} %constant_dynamic-slice_fusion.2), kind=kOutput, calls=%fused_computation.4.clone.1 | convolution fusion | flops 153092096 | bytes 311296 | tf_op jit(solution)/shard_map/while/body/eval_jaxpr/icj,ijk->ick/dot_general | solution.py:124
  100.8 2.7 %fusion.107 = f32[1,16,6,256]{3,2,1,0:T(8,128)S(1)} fusion(s32[16,256]{1,0:T(8,128)S(1)} %dynamic-slice_bitcast_fusion.2, f32[1,16,6,512]{3,1,2,0:T(8,128)S(1)} %constant_dynamic-slice_fusion.2), kind=kOutput, calls=%fused_computation.4.clone.1 | convolution fusion | flops 153092096 | bytes 311296 | tf_op jit(solution)/shard_map/while/body/eval_jaxpr/icj,ijk->ick/dot_general | solution.py:124
  103.6 0.9 constant_dynamic-slice_fusion.2
  104.6 2.7 %fusion.107 = f32[1,16,6,256]{3,2,1,0:T(8,128)S(1)} fusion(s32[16,256]{1,0:T(8,128)S(1)} %dynamic-slice_bitcast_fusion.2, f32[1,16,6,512]{3,1,2,0:T(8,128)S(1)} %constant_dynamic-slice_fusion.2), kind=kOutput, calls=%fused_computation.4.clone.1 | convolution fusion | flops 153092096 | bytes 311296 | tf_op jit(solution)/shard_map/while/body/eval_jaxpr/icj,ijk->ick/dot_general | solution.py:124
  110.1 5.6 %fusion.9 = f32[12,12,16,16]{0,1,3,2:T(8,128)S(1)} fusion(f32[12,16,16,256]{3,2,1,0:T(8,128)S(1)} %broadcast_multiply_fusion), kind=kOutput, calls=%fused_computation.13 | convolution fusion | flops 113246208 | bytes 3293184 | tf_op jit(solution)/shard_map/anks,bnks->abnk/dot_general | solution.py:34
  115.8 1.7 %fusion.98 = (f32[6,6,16,16]{0,1,3,2:T(8,128)}, f32[6,6,16,16]{0,1,3,2:T(8,128)}) fusion(f32[12,12,16,16]{0,1,3,2:T(8,128)S(1)} %fusion.9), kind=kLoop, calls=%fused_computation.184 | loop fusion | bytes 147456 | tf_op jit(solution)/shard_map/slice | solution.py:40
  117.5 2.0 %copy.48 = f32[6,6,16,16]{3,2,1,0:T(8,128)S(1)} copy(f32[6,6,16,16]{0,1,3,2:T(8,128)} %get-tuple-element.108) | data formatting | bytes 73728 | tf_op jit(solution)/shard_map/slice | solution.py:38
  120.4 6.6 %fusion.5 = f32[16,16,1,12]{3,2,1,0:T(1,128)S(1)} fusion(f32[12,16,16,256]{3,2,1,0:T(8,128)S(1)} %broadcast_multiply_fusion, f32[16,16,256,1]{2,1,0,3:T(8,128)} %get-tuple-element.105), kind=kOutput, calls=%fused_computation.9 | convolution fusion | flops 9437184 | bytes 3420160 | tf_op jit(solution)/shard_map/anks,nks->ank/dot_general | solution.py:35
  128.0 5.9 %all-to-all-start.1 = ((f32[16,1,672]{2,1,0:T(1,128)}), f32[16,1,672]{2,1,0:T(1,128)S(1)}, u32[]{:S(2)}, u32[]{:S(2)}) async-start(f32[16,1,672]{2,1,0:T(1,128)} %reshape.337), calls=%async_computation.1 | async-start | bytes 98304 | tf_op jit(solution)/shard_map/all_to_all | solution.py:140
  133.8 1.0 slice_convert_fusion
  135.3 2.0 %copy.51 = f32[6,6,16,16]{3,2,1,0:T(8,128)S(1)} copy(f32[6,6,16,16]{0,1,3,2:T(8,128)} %get-tuple-element.107) | data formatting | bytes 73728 | tf_op jit(solution)/shard_map/slice | solution.py:40
  137.6 3.8 %all-to-all-done.1 = f32[16,1,672]{2,1,0:T(1,128)S(1)} async-done(((f32[16,1,672]{2,1,0:T(1,128)}), f32[16,1,672]{2,1,0:T(1,128)S(1)}, u32[]{:S(2)}, u32[]{:S(2)}) %all-to-all-start.1) | async-done | bytes 43040 | tf_op jit(solution)/shard_map/all_to_all | solution.py:140
  143.2 3.4 %psum.7 = f32[42,64]{1,0:T(8,128)S(1)} all-reduce(f32[42,64]{1,0:T(8,128)S(1)} %convolution_add_fusion), channel_id=1, replica_groups=mesh['grp'=2,'tile'=16] {'grp'}, use_global_device_ids=true, to_apply=%region_5.6 | all-reduce | flops 2688 | bytes 21504 | tf_op jit(solution)/shard_map/psum | solution.py:152
  (87 shorter events, 13.7 us)
Async XLA Ops:
  5.1 12.4 %copy-start.2 = (f32[3,32768]{1,0:T(4,128)S(1)}, f32[3,32768]{1,0:T(4,128)}, u32[]{:S(2)}) copy-start(f32[3,32768]{1,0:T(4,128)} %param.13) | copy-start | bytes 1179652
  9.2 32.7 %all-to-all-start = ((f32[4,16,16,256]{3,2,0,1:T(8,128)}), f32[4,16,16,256]{3,2,0,1:T(8,128)S(1)}, u32[]{:S(2)}, u32[]{:S(2)}) async-start(f32[4,16,16,256]{3,2,0,1:T(8,128)} %pad_maximum_fusion), calls=%async_computation | async-start | bytes 2097152 | tf_op jit(solution)/shard_map/all_to_all | solution.py:108
  41.9 67.0 %copy-start = (f32[4,16,16,256]{3,2,0,1:T(8,128)}, f32[4,16,16,256]{3,2,0,1:T(8,128)S(1)}, u32[]{:S(2)}) copy-start(f32[4,16,16,256]{3,2,0,1:T(8,128)S(1)} %all-to-all-done) | copy-start | bytes 3145732
  120.4 6.7 %copy-start.1 = (f32[36,16,16]{0,2,1:T(8,128)S(1)}, f32[36,16,16]{0,2,1:T(8,128)}, u32[]{:S(2)}) copy-start(f32[36,16,16]{0,2,1:T(8,128)} %copy.50) | copy-start | bytes 110596
  128.0 13.4 %all-to-all-start.1 = ((f32[16,1,672]{2,1,0:T(1,128)}), f32[16,1,672]{2,1,0:T(1,128)S(1)}, u32[]{:S(2)}, u32[]{:S(2)}) async-start(f32[16,1,672]{2,1,0:T(1,128)} %reshape.337), calls=%async_computation.1 | async-start | bytes 98304 | tf_op jit(solution)/shard_map/all_to_all | solution.py:140
where the time goes:
time: 148 us; the launch traced here: 147 us
  matrix products  63.2 us (43%)
  local copies, waits for them, and re-layouts  26.6 us (18%)
  waiting for transfers between devices  25.9 us (18%)
  starting transfers between devices  14.2 us (10%)
  other arithmetic  13 us (9%)
  blocking collectives  3.42 us (2%)
    dot_general x16, matrix products, select(): return jnp.einsum('icj,ijk->ick', table_part, chooser, precision=PRECISE)  43.9 us
    all_to_all x1, waiting for transfers between devices, body(): lax.all_to_all(outgoing, 'tile', split_axis=1, concat_axis=1, tiled=True)  22.1 us
    dynamic_slice x16, local copies, waits for them, and re-layouts, body(): lax.map(select, (block_tables.reshape(items // group, group, 6, TARGET_PT...  15.1 us
    all_to_all x1, starting transfers between devices, body(): lax.all_to_all(outgoing, 'tile', split_axis=1, concat_axis=1, tiled=True)  8.34 us
    dot_general x1, matrix products, pair_terms(): gradient = jnp.einsum('anks,nks->ank', jacobian, misfit, precision=PRECISE)  6.57 us
    all_to_all x1, starting transfers between devices, body(): lax.all_to_all(mine, 'tile', split_axis=1, concat_axis=1, tiled=True)  5.89 us
    dot_general x1, matrix products, pair_terms(): jnp.einsum('anks,bnks->abnk', jacobian, jacobian, precision=PRECISE)  5.64 us
    dot_general x1, matrix products, body(): jnp.dot(scan_pick, tables, precision=PRECISE).reshape(items, 6, TARGET_PTS)  4.73 us
  transfers between devices with their start and end apart: 2, of which 2 were waited for; matrix products, arithmetic and copies ran while one was open for 4% of the time, Pallas kernels for 0%

commit v1 on v0

v1 whole, which is shorter than its diff:
```python
import functools

import jax
import jax.numpy as jnp
from jax import lax
from jax.experimental import pallas as pl
from jax.experimental.pallas import tpu as pltpu
from jax.sharding import PartitionSpec as P

SCANS_DEV = 64
TARGET_PTS = 512
DAMPING = 0.1
LANES = 128
PRECISE = lax.Precision.HIGHEST
MESH = pl.DeviceIdType.MESH
VMEM = pl.BlockSpec(memory_space=pltpu.VMEM)
SMEM = pl.BlockSpec(memory_space=pltpu.SMEM)


def pack_kernel(dest, chosen, sp, mt, pts, idx, seg, count):
    tiles, _, cap, points = pts.shape
    blocks = dest.shape[0]
    per_scan = blocks // SCANS_DEV
    idx[...] = jnp.full(idx.shape, -1, jnp.int32)

    def clear(t, c):
        count[t] = 0
        return c

    lax.fori_loop(0, tiles, clear, 0)

    def unset(s, c):
        seg[0, s] = -1
        return c

    lax.fori_loop(0, tiles * cap, unset, 0, unroll=8)

    def step(b, c):
        d = dest[b]
        r = count[d]
        count[d] = r + 1
        seg[0, d * cap + r] = b // per_scan
        cols = pl.ds(pl.multiple_of(b * points, points), points)
        for a in range(3):
            pts[d, a, pl.ds(r, 1), :] = sp[0, a : a + 1, cols]
        idx[d, pl.ds(r, 1), :] = mt[0:1, cols] + chosen[0, b] * TARGET_PTS
        return c

    lax.fori_loop(0, blocks, step, 0, unroll=4)


def greet_tiles(tiles, me, extra):
    barrier = pltpu.get_barrier_semaphore()

    def one(k, c):
        pl.semaphore_signal(
            barrier, inc=1, device_id={"tile": lax.rem(me + k, tiles)}, device_id_type=MESH
        )
        return c

    lax.fori_loop(1, tiles, one, 0)
    if extra:
        pl.semaphore_signal(
            barrier, inc=1, device_id={"grp": 1 - lax.axis_index("grp")}, device_id_type=MESH
        )
    pl.semaphore_wait(barrier, tiles - 1 + extra)


def exchange_kernel(pts, idx, got_pts, got_idx, ps, pr, qs, qr, ls):
    tiles = pts.shape[0]
    me = lax.axis_index("tile")
    greet_tiles(tiles, me, 0)

    def copies(to, frm):
        return (
            pltpu.make_async_remote_copy(
                idx.at[to], got_idx.at[frm], qs.at[to], qr.at[frm], {"tile": to}, MESH
            ),
            pltpu.make_async_remote_copy(
                pts.at[to], got_pts.at[frm], ps.at[to], pr.at[frm], {"tile": to}, MESH
            ),
        )

    def send(k, c):
        for copy in copies(lax.rem(me + k, tiles), me):
            copy.start()
        return c

    lax.fori_loop(1, tiles, send, 0)
    mine = (
        pltpu.make_async_copy(idx.at[me], got_idx.at[me], ls.at[0]),
        pltpu.make_async_copy(pts.at[me], got_pts.at[me], ls.at[1]),
    )
    for copy in mine:
        copy.start()
    for copy in mine:
        copy.wait()

    def finish(k, c):
        to = lax.rem(me + k, tiles)
        frm = lax.rem(me + tiles - k, tiles)
        for copy in copies(to, frm):
            copy.wait_send()
        for copy in copies(to, frm):
            copy.wait_recv()
        return c

    lax.fori_loop(1, tiles, finish, 0)


def cross(u, v):
    return [
        u[1] * v[2] - u[2] * v[1],
        u[2] * v[0] - u[0] * v[2],
        u[0] * v[1] - u[1] * v[0],
    ]


def upper(vec):
    return [(a, b) for a in range(6) for b in range(a, 6)]


def compute_kernel(ids, pts, idx, tp, tn, own, far, table, picked):
    tiles, _, cap, points = pts.shape

    def fill(s, c):
        cols = pl.ds(pl.multiple_of(s * TARGET_PTS, TARGET_PTS), TARGET_PTS)
        table[s, 0:3, :] = tp[:, cols]
        table[s, 3:6, :] = tn[:, cols]
        return c

    lax.fori_loop(0, SCANS_DEV, fill, 0, unroll=4)
    lane = lax.broadcasted_iota(jnp.int32, (8, LANES), 1)

    def group(i, c):
        d = i // (cap // 8)
        r0 = pl.multiple_of((i % (cap // 8)) * 8, 8)
        near = idx[d, pl.ds(r0, 8), :]
        for j in range(8):
            tab = table.at[jnp.maximum(ids[i * 8 + j], 0)]
            for h in range(points // LANES):
                at = jnp.broadcast_to(near[j : j + 1, h * LANES : (h + 1) * LANES], (8, LANES))
                low = at & (LANES - 1)
                high = (at >> 7) & (TARGET_PTS // LANES - 1)
                out = None
                for q in range(TARGET_PTS // LANES):
                    part = jnp.take_along_axis(
                        tab[:, q * LANES : (q + 1) * LANES],
                        low,
                        axis=1,
                        mode="promise_in_bounds",
                    )
                    out = part if out is None else jnp.where(high == q, part, out)
                picked[h, j * 8 : j * 8 + 8, :] = out
        halves = []
        for h in range(points // LANES):
            span = slice(h * LANES, (h + 1) * LANES)
            good = near[:, span] >= 0
            p = [jnp.where(good, pts[d, a, pl.ds(r0, 8), span], 0.0) for a in range(3)]
            q = [picked[h, pl.ds(a, 8, stride=8), :] for a in range(3)]
            n = [
                jnp.where(good, picked[h, pl.ds(3 + a, 8, stride=8), :], 0.0) for a in range(3)
            ]
            mis = n[0] * (p[0] - q[0]) + n[1] * (p[1] - q[1]) + n[2] * (p[2] - q[2])
            halves.append((cross(p, n) + n, cross(q, n) + n, mis))
        own_row = jnp.zeros((8, LANES), jnp.float32)
        far_row = jnp.zeros((8, LANES), jnp.float32)

        def total(make):
            acc = None
            for half in halves:
                acc = make(half) if acc is None else acc + make(half)
            return jnp.sum(acc, axis=1, keepdims=True)

        for f, (a, b) in enumerate(upper(6)):
            s = total(lambda v: v[0][a] * v[0][b])
            own_row = jnp.where(lane == f, s, own_row)
            if a < 3:
                s = total(lambda v: v[1][a] * v[1][b])
            far_row = jnp.where(lane == f, s, far_row)
        for a in range(6):
            s = total(lambda v: v[0][a] * v[2])
            own_row = jnp.where(lane == 21 + a, s, own_row)
            if a < 3:
                s = total(lambda v: v[1][a] * v[2])
            far_row = jnp.where(lane == 21 + a, -s, far_row)
        own[d, pl.ds(r0, 8), :] = own_row
        far[d, pl.ds(r0, 8), :] = far_row
        return c

    lax.fori_loop(0, tiles * (cap // 8), group, 0)


def solve_rows(rows):
    entries = {}
    for f, (a, b) in enumerate(upper(6)):
        entries[a, b] = rows[f]
    traced = entries[0, 0]
    for a in range(1, 6):
        traced = traced + entries[a, a]
    shift_by = DAMPING * traced / 6.0
    for a in range(6):
        entries[a, a] = entries[a, a] + shift_by
    values = [-rows[21 + a] for a in range(6)]
    for k in range(6):
        for a in range(k + 1, 6):
            factor = entries[k, a] / entries[k, k]
            for b in range(a, 6):
                entries[a, b] = entries[a, b] - factor * entries[k, b]
            values[a] = values[a] - factor * values[k]
    result = [None] * 6
    for a in range(5, -1, -1):
        running = values[a]
        for b in range(a + 1, 6):
            running = running - entries[a, b] * result[b]
        result[a] = running / entries[a, a]
    return result


def return_kernel(own, far, seg, ids, out, back, tot, partner, ss, rs, gs, gr):
    tiles, cap, _ = own.shape
    me = lax.axis_index("tile")
    greet_tiles(tiles, me, 1)

    def copy(to, frm):
        return pltpu.make_async_remote_copy(
            own.at[to], back.at[frm], ss.at[to], rs.at[frm], {"tile": to}, MESH
        )

    def send(k, c):
        copy(lax.rem(me + k, tiles), me).start()
        return c

    lax.fori_loop(1, tiles, send, 0)
    back[me] = own[me]
    scan = lax.broadcasted_iota(jnp.int32, (SCANS_DEV, tiles * cap), 0)
    to_far = (scan == ids[...]).astype(jnp.float32)
    to_own = (scan == seg[...]).astype(jnp.float32)
    sums = jnp.dot(
        to_far,
        far[...].reshape(tiles * cap, LANES),
        precision=PRECISE,
        preferred_element_type=jnp.float32,
    )

    def finish(k, c):
        copy(lax.rem(me + k, tiles), lax.rem(me + tiles - k, tiles)).wait()
        return c

    lax.fori_loop(1, tiles, finish, 0)
    sums = sums + jnp.dot(
        to_own,
        back[...].reshape(tiles * cap, LANES),
        precision=PRECISE,
        preferred_element_type=jnp.float32,
    )
    tot[...] = sums
    swap = pltpu.make_async_remote_copy(
        tot, partner, gs, gr, {"grp": 1 - lax.axis_index("grp")}, MESH
    )
    swap.start()
    swap.wait()
    full = jnp.transpose(tot[...] + partner[...])
    for a, row in enumerate(solve_rows([full[f : f + 1, :] for f in range(27)])):
        out[a : a + 1, :] = row


def body(source_points, intersection, target_scan, matches, target_points, target_normals):
    tiles = lax.axis_size("tile")
    blocks = intersection.shape[1]
    points = source_points.shape[2] // blocks
    cap = -(-(2 * blocks // tiles) // 8) * 8
    f32, i32 = jnp.float32, jnp.int32
    shape = jax.ShapeDtypeStruct
    dma = pltpu.SemaphoreType.DMA
    pts, idx, seg = pl.pallas_call(
        pack_kernel,
        out_shape=(
            shape((tiles, 3, cap, points), f32),
            shape((tiles, cap, points), i32),
            shape((1, tiles * cap), i32),
        ),
        in_specs=[SMEM, SMEM, VMEM, VMEM],
        out_specs=(VMEM, VMEM, SMEM),
        scratch_shapes=[pltpu.SMEM((tiles,), i32)],
        name="pack",
    )(intersection.reshape(blocks), target_scan, source_points, matches)
    pts, idx = pl.pallas_call(
        exchange_kernel,
        out_shape=(shape(pts.shape, f32), shape(idx.shape, i32)),
        in_specs=[VMEM, VMEM],
        out_specs=(VMEM, VMEM),
        scratch_shapes=[dma((tiles,)), dma((tiles,)), dma((tiles,)), dma((tiles,)), dma((2,))],
        compiler_params=pltpu.CompilerParams(collective_id=0, has_side_effects=True),
        name="exchange",
    )(pts, idx)
    lead = idx[:, :, 0].reshape(1, tiles * cap)
    ids = jnp.where(lead >= 0, lead // TARGET_PTS, -1)
    own, far = pl.pallas_call(
        compute_kernel,
        out_shape=(shape((tiles, cap, LANES), f32), shape((tiles, cap, LANES), f32)),
        in_specs=[SMEM, VMEM, VMEM, VMEM, VMEM],
        out_specs=(VMEM, VMEM),
        scratch_shapes=[
            pltpu.VMEM((SCANS_DEV, 8, TARGET_PTS), f32),
            pltpu.VMEM((points // LANES, 64, LANES), f32),
        ],
        name="compute",
    )(ids.reshape(tiles * cap), pts, idx, target_points, target_normals)
    return pl.pallas_call(
        return_kernel,
        out_shape=shape((6, SCANS_DEV), f32),
        in_specs=[VMEM, VMEM, VMEM, VMEM],
        out_specs=VMEM,
        scratch_shapes=[
            pltpu.VMEM((tiles, cap, LANES), f32),
            pltpu.VMEM((SCANS_DEV, LANES), f32),
            pltpu.VMEM((SCANS_DEV, LANES), f32),
            dma((tiles,)),
            dma((tiles,)),
            dma,
            dma,
        ],
        compiler_params=pltpu.CompilerParams(collective_id=1, has_side_effects=True),
        name="giveback",
    )(own, far, seg, ids)


def solution(mesh):
    in_specs = (
        P("grp", None, "tile"),
        P("grp", "tile", None),
        P("grp", "tile"),
        P("grp", "tile"),
        P(None, "tile"),
        P(None, "tile"),
    )
    out_specs = P(None, "tile")
    return jax.shard_map(body, mesh=mesh, in_specs=in_specs, out_specs=out_specs, check_vma=False)
```

time: 148 us -> 67.6 us (0.46)
  matrix products: 63.2 us -> 0 us
  Pallas kernels: 0 us -> 61.4 us
  waiting for transfers between devices: 25.9 us -> 0 us
  local copies, waits for them, and re-layouts: 26.6 us -> 4.72 us
  starting transfers between devices: 14.2 us -> 0 us
  other arithmetic: 13 us -> 1.18 us
  blocking collectives: 3.42 us -> 0 us
    dot_general x25 -> x0, matrix products: 63.2 us -> none  [the longest x16 43.9 us: select(): return jnp.einsum('icj,ijk->ick', table_part, chooser, precision=PRECISE)]
    pallas_call x0 -> x4, Pallas kernels: none -> 61.4 us  [the longest x1 26.6 us: body(): pl.pallas_call(exchange_kernel, out_shape=(shape(pts.shape, f32), shape(i...]
    all_to_all x2 -> x0, waiting for transfers between devices: 25.9 us -> none  [the longest x1 22.1 us: body(): lax.all_to_all(outgoing, 'tile', split_axis=1, concat_axis=1, tiled=True)]
    dynamic_slice x16 -> x0, local copies, waits for them, and re-layouts: 15.1 us -> none  [body(): lax.map(select, (block_tables.reshape(items // group, group, 6, TARGET_PT...]
    all_to_all x2 -> x0, starting transfers between devices: 14.2 us -> none  [the longest x1 8.34 us: body(): lax.all_to_all(outgoing, 'tile', split_axis=1, concat_axis=1, tiled=True)]
    slice x8 -> x1, local copies, waits for them, and re-layouts: 6.61 us -> 1.25 us  [body(): lead = idx[:, :, 0].reshape(1, tiles * cap)]
    unnamed x6 -> x0, other arithmetic: 4.35 us -> none
    psum x1 -> x0, blocking collectives: 3.42 us -> none  [body(): totals = lax.psum(local_sums, 'grp')]
  transfers between devices with their start and end apart: 2 -> 0, of which waited for: 2 -> 0; matrix products, arithmetic and copies ran while one was open for 4% -> 0% of each run, Pallas kernels for 0% -> 0%
where the time goes in v1:
time: 67.6 us; the launch traced here: 67.3 us
  Pallas kernels  61.4 us (91%)
  local copies, waits for them, and re-layouts  4.72 us (7%)
  other arithmetic  1.18 us (2%)
    pallas_call x1, Pallas kernels, body(): pl.pallas_call(exchange_kernel, out_shape=(shape(pts.shape, f32), shape(i...  26.6 us
    pallas_call x1, Pallas kernels, body(): pl.pallas_call(return_kernel, out_shape=shape((6, SCANS_DEV), f32), in_sp...  17 us
    pallas_call x1, Pallas kernels, body(): pl.pallas_call(compute_kernel, out_shape=(shape((tiles, cap, LANES), f32)...  13.6 us
    pallas_call x1, Pallas kernels, body(): pl.pallas_call(pack_kernel, out_shape=(shape((tiles, 3, cap, points), f32...  4.26 us
    unnamed x2, local copies, waits for them, and re-layouts  3.31 us

profile of v1, /device:TPU:0, one launch (start us, length us, event | category | flops | bytes accessed | tf_op | source)
XLA Modules:
  0.0 67.3 jit_solution(367937910280324917)
XLA Ops:
  0.0 2.0 %copy.8.sp = f32[1,3,32768]{2,1,0:T(4,128)} copy(f32[1,3,32768]{2,0,1:T(1,128)} %param.6) | data formatting | bytes 786432 | tf_op args[0]
  2.1 4.3 %pack.1 = (f32[16,3,16,256]{3,2,1,0:T(8,128)}, s32[16,16,256]{2,1,0:T(8,128)}, s32[1,256]{1,0:T(1,128)}) custom-call(s32[128]{0:T(128)} %bitcast.1, s32[1,128]{1,0:T(1,128)} %chosen.1, f32[1,3,32768]{2,1,0:T(4,128)} %copy.8.sp, s32[1,32768]{1,0:T(1,128)} %mt.1), custom_call_target="tpu_custom_call" | custom-call | tf_op jit(solution)/shard_map/pack/pallas_call | solution.py:276
  6.3 26.6 %exchange.1 = (f32[16,3,16,256]{3,2,1,0:T(8,128)}, s32[16,16,256]{2,1,0:T(8,128)}) custom-call(f32[16,3,16,256]{3,2,1,0:T(8,128)} %get-tuple-element.12.pts, s32[16,16,256]{2,1,0:T(8,128)} %get-tuple-element.13.idx), custom_call_target="tpu_custom_call" | custom-call | tf_op jit(solution)/shard_map/exchange/pallas_call | solution.py:288
  32.9 1.2 %slice_reduce_fusion = s32[16,16]{1,0:T(8,128)S(1)} fusion(s32[16,16,256]{2,1,0:T(8,128)} %get-tuple-element.14.idx), kind=kLoop, calls=%fused_computation | loop fusion | bytes 2048 | tf_op jit(solution)/shard_map/slice | solution.py:297
  34.2 0.1 reshape_squeeze.6
  34.3 0.1 reshape_squeeze.5
  34.3 0.6 compare_select_fusion.4.ids
  35.0 13.6 %compute.1 = (f32[16,16,128]{2,1,0:T(8,128)}, f32[16,16,128]{2,1,0:T(8,128)}) custom-call(s32[256]{0:T(256)} %compare_select_fusion.4.ids, f32[16,3,16,256]{3,2,1,0:T(8,128)} %get-tuple-element.15.pts, s32[16,16,256]{2,1,0:T(8,128)} %get-tuple-element.14.idx, f32[3,32768]{1,0:T(4,128)} %tp.1, f32[3,32768]{1,0:T(4,128)} %tn.1), custom_call_target="tpu_custom_call" | custom-call | tf_op jit(solution)/shard_map/compute/pallas_call | solution.py:299
  48.5 0.6 compare_select_fusion.ids
  49.1 17.0 %giveback.1 = f32[6,64]{1,0:T(8,128)} custom-call(f32[16,16,128]{2,1,0:T(8,128)} %get-tuple-element.16.own, f32[16,16,128]{2,1,0:T(8,128)} %get-tuple-element.17.far, s32[1,256]{1,0:T(1,128)} %get-tuple-element.18.seg, s32[1,256]{1,0:T(1,128)} %compare_select_fusion.ids), custom_call_target="tpu_custom_call" | custom-call | tf_op jit(solution)/shard_map/giveback/pallas_call | solution.py:310
  66.1 1.3 %copy.10 = f32[6,64]{1,0:T(8,128)} copy(f32[6,64]{1,0:T(8,128)} %giveback.1) | data formatting | bytes 3072

commit v2 on v1

v2 whole, which is shorter than its diff:
```python
import jax
import jax.numpy as jnp
from jax import lax
from jax.experimental import pallas as pl
from jax.experimental.pallas import tpu as pltpu
from jax.sharding import PartitionSpec as P

SCANS_DEV = 64
TARGET_PTS = 512
DAMPING = 0.1
LANES = 128
PAIR = 32
PRECISE = lax.Precision.HIGHEST
MESH = pl.DeviceIdType.MESH
VMEM = pl.BlockSpec(memory_space=pltpu.VMEM)
SMEM = pl.BlockSpec(memory_space=pltpu.SMEM)


def pack_kernel(dest, chosen, sp, mt, pts, idx, ids, seg, count):
    tiles, _, cap, points = pts.shape
    blocks = dest.shape[0]
    per_scan = blocks // SCANS_DEV
    idx[...] = jnp.full(idx.shape, -1, jnp.int32)

    def clear(t, c):
        count[t] = 0
        for r in range(cap):
            ids[t, 0, r] = -1
            seg[r // 8, t * 8 + r % 8] = -1
        return c

    lax.fori_loop(0, tiles, clear, 0)

    def step(b, c):
        d = dest[b]
        r = count[d]
        count[d] = r + 1
        seg[r // 8, d * 8 + r % 8] = b // per_scan
        ids[d, 0, r] = chosen[0, b]
        cols = pl.ds(pl.multiple_of(b * points, points), points)
        for a in range(3):
            pts[d, a, pl.ds(r, 1), :] = sp[0, a : a + 1, cols]
        idx[d, pl.ds(r, 1), :] = mt[0:1, cols]
        return c

    lax.fori_loop(0, blocks, step, 0, unroll=4)


def near_first(tiles, me, start, act):
    def one(j, c):
        k = (j + 1) // 2
        t = me + k * (2 * (j % 2) - 1)

        @pl.when((t >= 0) & (t < tiles))
        def _():
            act(t, j)

        return c

    lax.fori_loop(start, 2 * tiles - 1, one, 0)


def cross(u, v):
    return [
        u[1] * v[2] - u[2] * v[1],
        u[2] * v[0] - u[0] * v[2],
        u[0] * v[1] - u[1] * v[0],
    ]


def upper(vec):
    return [(a, b) for a in range(6) for b in range(a, 6)]


def main_kernel(
    pts, idx, ids, seg, tp, tn, out,
    got_pts, got_idx, got_ids, named, table, picked, own, far, back, tot, partner,
    ps, pr, qs, qr, js, jr, ss, rs, ls, gs, gr,
):
    tiles, _, cap, points = pts.shape
    me = lax.axis_index("tile")
    other = 1 - lax.axis_index("grp")
    barrier = pltpu.get_barrier_semaphore()

    def greet(k, c):
        to = lax.rem(me + k, tiles)
        pl.semaphore_signal(barrier, inc=1, device_id={"tile": to}, device_id_type=MESH)
        return c

    lax.fori_loop(1, tiles, greet, 0)
    pl.semaphore_signal(barrier, inc=1, device_id={"grp": other}, device_id_type=MESH)
    pl.semaphore_wait(barrier, tiles)

    def remote(src, dst, send, recv, to, frm):
        return pltpu.make_async_remote_copy(
            src.at[to], dst.at[frm], send.at[to], recv.at[frm], {"tile": to}, MESH
        )

    def id_copy(to, frm):
        return remote(ids, got_ids, js, jr, to, frm)

    def idx_copy(to, frm):
        return remote(idx, got_idx, qs, qr, to, frm)

    def pts_copy(to, frm):
        return remote(pts, got_pts, ps, pr, to, frm)

    def own_copy(to, frm):
        return remote(own, back, ss, rs, to, frm)

    near_first(tiles, me, 1, lambda t, j: id_copy(t, me).start())

    def send(t, j):
        idx_copy(t, me).start()
        pts_copy(t, me).start()

    near_first(tiles, me, 1, send)
    mine = [
        pltpu.make_async_copy(src.at[me], dst.at[me], ls.at[i])
        for i, (src, dst) in enumerate(((ids, got_ids), (idx, got_idx), (pts, got_pts)))
    ]
    for copy in mine:
        copy.start()

    def fill(s, c):
        cols = pl.ds(pl.multiple_of(s * TARGET_PTS, TARGET_PTS), TARGET_PTS)
        table[s, 0:3, :] = tp[:, cols]
        table[s, 3:6, :] = tn[:, cols]
        return c

    lax.fori_loop(0, SCANS_DEV, fill, 0, unroll=4)
    tot[...] = jnp.zeros(tot.shape, jnp.float32)
    for copy in mine:
        copy.wait()
    near_first(tiles, me, 1, lambda t, j: id_copy(t, t).wait_recv())
    load_ids = pltpu.make_async_copy(got_ids, named, ls.at[3])
    load_ids.start()
    load_ids.wait()
    lane = lax.broadcasted_iota(jnp.int32, (8, LANES), 1)
    scan = lax.broadcasted_iota(jnp.int32, (SCANS_DEV, cap), 0)

    def group(d, g):
        r0 = g * 8
        near = got_idx[d, r0 : r0 + 8, :]
        for j in range(8):
            tab = table.at[jnp.maximum(named[d, 0, r0 + j], 0)]
            for h in range(points // LANES):
                at = jnp.broadcast_to(near[j : j + 1, h * LANES : (h + 1) * LANES], (8, LANES))
                low = at & (LANES - 1)
                high = (at >> 7) & (TARGET_PTS // LANES - 1)
                res = None
                for q in range(TARGET_PTS // LANES):
                    part = jnp.take_along_axis(
                        tab[:, q * LANES : (q + 1) * LANES],
                        low,
                        axis=1,
                        mode="promise_in_bounds",
                    )
                    res = part if res is None else jnp.where(high == q, part, res)
                picked[g, h, j * 8 : j * 8 + 8, :] = res
        halves = []
        for h in range(points // LANES):
            span = slice(h * LANES, (h + 1) * LANES)
            good = near[:, span] >= 0
            p = [
                jnp.where(good, got_pts[d, a, r0 : r0 + 8, span], 0.0) for a in range(3)
            ]
            q = [picked[g, h, pl.ds(a, 8, stride=8), :] for a in range(3)]
            n = [
                jnp.where(good, picked[g, h, pl.ds(3 + a, 8, stride=8), :], 0.0)
                for a in range(3)
            ]
            mis = n[0] * (p[0] - q[0]) + n[1] * (p[1] - q[1]) + n[2] * (p[2] - q[2])
            halves.append((cross(p, n) + n, cross(q, n) + n, mis))
        own_row = jnp.zeros((8, LANES), jnp.float32)
        far_row = jnp.zeros((8, LANES), jnp.float32)

        def total(make):
            acc = None
            for half in halves:
                acc = make(half) if acc is None else acc + make(half)
            return jnp.sum(acc, axis=1, keepdims=True)

        for f, (a, b) in enumerate(upper(6)):
            s = total(lambda v: v[0][a] * v[0][b])
            own_row = jnp.where(lane == PAIR * g + f, s, own_row)
            if a < 3:
                s = total(lambda v: v[1][a] * v[1][b])
            far_row = jnp.where(lane == f, s, far_row)
        for a in range(6):
            s = total(lambda v: v[0][a] * v[2])
            own_row = jnp.where(lane == PAIR * g + 21 + a, s, own_row)
            if a < 3:
                s = total(lambda v: v[1][a] * v[2])
            far_row = jnp.where(lane == 21 + a, -s, far_row)
        far[r0 : r0 + 8, :] = far_row
        return own_row

    def work(t, j):
        @pl.when(j > 0)
        def _():
            idx_copy(t, t).wait_recv()
            pts_copy(t, t).wait_recv()

        row = group(t, 0)
        for g in range(1, cap // 8):
            row = row + group(t, g)
        own[t] = row

        @pl.when(j == 0)
        def _():
            back[me] = own[me]

        @pl.when(j > 0)
        def _():
            own_copy(t, me).start()

        here = (scan == got_ids[t][:, :cap]).astype(jnp.float32)
        tot[...] += jnp.dot(
            here, far[...], precision=PRECISE, preferred_element_type=jnp.float32
        )

    near_first(tiles, me, 0, work)
    near_first(tiles, me, 1, lambda t, j: own_copy(t, t).wait_recv())
    wide = lax.broadcasted_iota(jnp.int32, (SCANS_DEV, tiles * 8), 0)
    rows = back[...].reshape(tiles * 8, LANES)
    sums = tot[...]
    for g in range(cap // 8):
        here = (wide == seg[g : g + 1, :]).astype(jnp.float32)
        part = jnp.dot(here, rows, precision=PRECISE, preferred_element_type=jnp.float32)
        if g > 0:
            part = pltpu.roll(part, LANES - PAIR * g, 1)
        sums = sums + part
    tot[...] = sums
    swap = pltpu.make_async_remote_copy(tot, partner, gs, gr, {"grp": other}, MESH)
    swap.start()

    def drain(t, j):
        for copy in (id_copy, idx_copy, pts_copy, own_copy):
            copy(t, me).wait_send()

    near_first(tiles, me, 1, drain)
    swap.wait()
    out[...] = jnp.transpose(tot[...] + partner[...])[:PAIR]


def solve_rows(rows):
    entries = {}
    for f, (a, b) in enumerate(upper(6)):
        entries[a, b] = rows[f]
    traced = entries[0, 0]
    for a in range(1, 6):
        traced = traced + entries[a, a]
    shift_by = DAMPING * traced / 6.0
    for a in range(6):
        entries[a, a] = entries[a, a] + shift_by
    values = [-rows[21 + a] for a in range(6)]
    for k in range(6):
        for a in range(k + 1, 6):
            factor = entries[k, a] / entries[k, k]
            for b in range(a, 6):
                entries[a, b] = entries[a, b] - factor * entries[k, b]
            values[a] = values[a] - factor * values[k]
    result = [None] * 6
    for a in range(5, -1, -1):
        running = values[a]
        for b in range(a + 1, 6):
            running = running - entries[a, b] * result[b]
        result[a] = running / entries[a, a]
    return result


def body(source_points, intersection, target_scan, matches, target_points, target_normals):
    tiles = lax.axis_size("tile")
    blocks = intersection.shape[1]
    points = source_points.shape[2] // blocks
    cap = -(-(2 * blocks // tiles) // 8) * 8
    f32, i32 = jnp.float32, jnp.int32
    shape = jax.ShapeDtypeStruct
    many = pltpu.SemaphoreType.DMA((tiles,))
    pts_t, idx_t = (tiles, 3, cap, points), (tiles, cap, points)
    ids_t, sums_t = (tiles, 1, LANES), (SCANS_DEV, LANES)
    pts, idx, ids, seg = pl.pallas_call(
        pack_kernel,
        out_shape=(
            shape(pts_t, f32),
            shape(idx_t, i32),
            shape(ids_t, i32),
            shape((cap // 8, tiles * 8), i32),
        ),
        in_specs=[SMEM, SMEM, VMEM, VMEM],
        out_specs=(VMEM, VMEM, SMEM, SMEM),
        scratch_shapes=[pltpu.SMEM((tiles,), i32)],
        name="pack",
    )(intersection.reshape(blocks), target_scan, source_points, matches)
    rows = pl.pallas_call(
        main_kernel,
        out_shape=shape((PAIR, SCANS_DEV), f32),
        in_specs=[VMEM] * 6,
        out_specs=VMEM,
        scratch_shapes=[
            pltpu.VMEM(pts_t, f32),
            pltpu.VMEM(idx_t, i32),
            pltpu.VMEM(ids_t, i32),
            pltpu.SMEM(ids_t, i32),
            pltpu.VMEM((SCANS_DEV, 8, TARGET_PTS), f32),
            pltpu.VMEM((cap // 8, points // LANES, 64, LANES), f32),
            pltpu.VMEM((tiles, 8, LANES), f32),
            pltpu.VMEM((cap, LANES), f32),
            pltpu.VMEM((tiles, 8, LANES), f32),
            pltpu.VMEM(sums_t, f32),
            pltpu.VMEM(sums_t, f32),
        ]
        + [many] * 8
        + [pltpu.SemaphoreType.DMA((4,)), pltpu.SemaphoreType.DMA, pltpu.SemaphoreType.DMA],
        compiler_params=pltpu.CompilerParams(collective_id=0, has_side_effects=True),
        name="main",
    )(pts, idx, ids, seg, target_points, target_normals)
    return jnp.stack(solve_rows(rows))


def solution(mesh):
    in_specs = (
        P("grp", None, "tile"),
        P("grp", "tile", None),
        P("grp", "tile"),
        P("grp", "tile"),
        P(None, "tile"),
        P(None, "tile"),
    )
    out_specs = P(None, "tile")
    return jax.shard_map(body, mesh=mesh, in_specs=in_specs, out_specs=out_specs, check_vma=False)
```

time: 67.6 us -> 56.1 us (0.83)
  Pallas kernels: 61.4 us -> 51.3 us
  local copies, waits for them, and re-layouts: 4.72 us -> 3.38 us
    pallas_call x4 -> x2, Pallas kernels: 61.4 us -> 51.3 us  [the longest x1 45.8 us: body(): pl.pallas_call(main_kernel, out_shape=shape((PAIR, SCANS_DEV), f32), in_s...]
    slice x1 -> x0, local copies, waits for them, and re-layouts: 1.25 us -> none  [body(): lead = idx[:, :, 0].reshape(1, tiles * cap)]
    select_n x2 -> x0, other arithmetic: 1.18 us -> none  [body(): ids = jnp.where(lead >= 0, lead // TARGET_PTS, -1)]
    sub x0 -> x3, other arithmetic: none -> 1.02 us  [the longest x2 1 us: solve_rows(): entries[a, b] = entries[a, b] - factor * entries[k, b]]
    unnamed x2 -> x3, local copies, waits for them, and re-layouts: 3.31 us -> 2.77 us
where the time goes in v2:
time: 56.1 us; the launch traced here: 55.8 us
  Pallas kernels  51.3 us (91%)
  local copies, waits for them, and re-layouts  3.38 us (6%)
  other arithmetic  1.07 us (2%)
    pallas_call x1, Pallas kernels, body(): pl.pallas_call(main_kernel, out_shape=shape((PAIR, SCANS_DEV), f32), in_s...  45.8 us
    pallas_call x1, Pallas kernels, body(): pl.pallas_call(pack_kernel, out_shape=(shape(pts_t, f32), shape(idx_t, i3...  5.5 us
    unnamed x3, local copies, waits for them, and re-layouts  2.77 us

profile of v2, /device:TPU:0, one launch (start us, length us, event | category | flops | bytes accessed | tf_op | source)
XLA Modules:
  0.0 55.8 jit_solution(1085429741254716964)
XLA Ops:
  0.0 2.1 %copy.7.sp = f32[1,3,32768]{2,1,0:T(4,128)} copy(f32[1,3,32768]{2,0,1:T(1,128)} %param.6) | data formatting | bytes 786432 | tf_op args[0]
  2.1 5.5 %pack.1 = (f32[16,3,16,256]{3,2,1,0:T(8,128)}, s32[16,16,256]{2,1,0:T(8,128)}, s32[16,1,128]{2,1,0:T(1,128)}, s32[2,128]{1,0:T(2,128)}) custom-call(s32[128]{0:T(128)} %bitcast.1, s32[1,128]{1,0:T(1,128)} %chosen.1, f32[1,3,32768]{2,1,0:T(4,128)} %copy.7.sp, s32[1,32768]{1,0:T(1,128)} %mt.1), custom_call_target="tpu_custom_call" | custom-call | tf_op jit(solution)/shard_map/pack/pallas_call | solution.py:283
  7.6 45.8 %main.1 = f32[32,64]{1,0:T(8,128)} custom-call(f32[16,3,16,256]{3,2,1,0:T(8,128)} %get-tuple-element.9.pts, s32[16,16,256]{2,1,0:T(8,128)} %get-tuple-element.10.idx, s32[16,1,128]{2,1,0:T(1,128)} %get-tuple-element.11.ids, s32[2,128]{1,0:T(2,128)} %get-tuple-element.12.seg, f32[3,32768]{1,0:T(4,128)} %tp.1, f32[3,32768]{1,0:T(4,128)} %tn.1), custom_call_target="tpu_custom_call" | custom-call | tf_op jit(solution)/shard_map/main/pallas_call | solution.py:296
  53.4 1.0 %multiply_subtract_fusion = (f32[1,64]{1,0:T(1,128)S(1)}, f32[1,64]{1,0:T(1,128)S(1)}, f32[1,64]{1,0:T(1,128)S(1)}, f32[1,64]{1,0:T(1,128)S(1)}, f32[1,64]{1,0:T...) fusion(f32[32,64]{1,0:T(8,128)} %main.1), kind=kLoop, calls=%fused_computation.6 | loop fusion | flops 3904 | bytes 9472 | tf_op jit(solution)/shard_map/sub | solution.py:262
  54.4 0.0 copy-start
  54.4 0.7 %copy-done = f32[32,64]{1,0:T(8,128)S(1)} copy-done((f32[32,64]{1,0:T(8,128)S(1)}, f32[32,64]{1,0:T(8,128)}, u32[]{:S(2)}) %copy-start) | copy-done | bytes 8216
  55.2 0.1 subtract_divide_fusion
  55.2 0.6 %stack.2 = f32[6,64]{1,0:T(8,128)} concatenate(f32[1,64]{1,0:T(1,128)S(1)} %get-tuple-element.13, f32[1,64]{1,0:T(1,128)S(1)} %get-tuple-element.14, f32[1,64]{1,0:T(1,128)S(1)} %get-tuple-element.15, f32[1,64]{1,0:T(1,128)S(1)} %get-tuple-element.16, f32[1,64]{1,0:T(1,128)S(1)} %get-tuple-element.17, f32[1,64]{1,0:T(1,128)S(1)} %get-tuple-element.18), dimensions={0} | concatenate | bytes 3072 | tf_op jit(solution)/shard_map/stack | solution.py:319
  (2 shorter events, 0.0 us)
Async XLA Ops:
  54.4 0.7 %copy-start = (f32[32,64]{1,0:T(8,128)S(1)}, f32[32,64]{1,0:T(8,128)}, u32[]{:S(2)}) copy-start(f32[32,64]{1,0:T(8,128)} %main.1) | copy-start | bytes 24580

commit v3 on v2

--- a/solution.py
+++ b/solution.py
@@ -16,15 +16,16 @@
 SMEM = pl.BlockSpec(memory_space=pltpu.SMEM)
 
 
-def pack_kernel(dest, chosen, sp, mt, pts, idx, ids, seg, count):
-    tiles, _, cap, points = pts.shape
+def plan_kernel(dest, chosen, block, ids, seg, count):
+    tiles = ids.shape[0]
     blocks = dest.shape[0]
+    cap = block.shape[0] // tiles
     per_scan = blocks // SCANS_DEV
-    idx[...] = jnp.full(idx.shape, -1, jnp.int32)
 
     def clear(t, c):
         count[t] = 0
         for r in range(cap):
+            block[t * cap + r] = -1
             ids[t, 0, r] = -1
             seg[r // 8, t * 8 + r % 8] = -1
         return c
@@ -37,10 +38,7 @@
         count[d] = r + 1
         seg[r // 8, d * 8 + r % 8] = b // per_scan
         ids[d, 0, r] = chosen[0, b]
-        cols = pl.ds(pl.multiple_of(b * points, points), points)
-        for a in range(3):
-            pts[d, a, pl.ds(r, 1), :] = sp[0, a : a + 1, cols]
-        idx[d, pl.ds(r, 1), :] = mt[0:1, cols]
+        block[d * cap + r] = b
         return c
 
     lax.fori_loop(0, blocks, step, 0, unroll=4)
@@ -73,8 +71,8 @@
 
 
 def main_kernel(
-    pts, idx, ids, seg, tp, tn, out,
-    got_pts, got_idx, got_ids, named, table, picked, own, far, back, tot, partner,
+    block, sp, mt, ids, seg, tp, tn, out,
+    pts, idx, got_pts, got_idx, got_ids, named, table, picked, own, far, back, tot, partner,
     ps, pr, qs, qr, js, jr, ss, rs, ls, gs, gr,
 ):
     tiles, _, cap, points = pts.shape
@@ -110,17 +108,40 @@
 
     near_first(tiles, me, 1, lambda t, j: id_copy(t, me).start())
 
-    def send(t, j):
-        idx_copy(t, me).start()
-        pts_copy(t, me).start()
-
-    near_first(tiles, me, 1, send)
-    mine = [
-        pltpu.make_async_copy(src.at[me], dst.at[me], ls.at[i])
-        for i, (src, dst) in enumerate(((ids, got_ids), (idx, got_idx), (pts, got_pts)))
-    ]
-    for copy in mine:
-        copy.start()
+    def pack(t, pts_to, idx_to):
+        for r in range(cap):
+            b = block[t * cap + r]
+            used = jnp.minimum(b, 0) + 1
+            for h in range(points // LANES):
+                span = slice(h * LANES, (h + 1) * LANES)
+                at = jnp.maximum(b, 0) * (points // LANES) + h
+                for a in range(3):
+                    pts_to[t, a, r : r + 1, span] = sp[a, at]
+                idx_to[t, r : r + 1, span] = mt[at] * used + (used - 1)
+
+    def at_step(j):
+        return me + (j + 1) // 2 * (2 * (j % 2) - 1)
+
+    def pack_send(j, c):
+        t = at_step(j)
+
+        @pl.when((j < 2 * tiles - 1) & (t >= 0) & (t < tiles))
+        def _():
+            pack(t, pts, idx)
+
+        u = at_step(j - 1)
+
+        @pl.when((j > 1) & (u >= 0) & (u < tiles))
+        def _():
+            idx_copy(u, me).start()
+            pts_copy(u, me).start()
+
+        return c
+
+    lax.fori_loop(1, 2 * tiles, pack_send, 0)
+    self_ids = pltpu.make_async_copy(ids.at[me], got_ids.at[me], ls.at[0])
+    self_ids.start()
+    pack(me, got_pts, got_idx)
 
     def fill(s, c):
         cols = pl.ds(pl.multiple_of(s * TARGET_PTS, TARGET_PTS), TARGET_PTS)
@@ -130,10 +151,9 @@
 
     lax.fori_loop(0, SCANS_DEV, fill, 0, unroll=4)
     tot[...] = jnp.zeros(tot.shape, jnp.float32)
-    for copy in mine:
-        copy.wait()
+    self_ids.wait()
     near_first(tiles, me, 1, lambda t, j: id_copy(t, t).wait_recv())
-    load_ids = pltpu.make_async_copy(got_ids, named, ls.at[3])
+    load_ids = pltpu.make_async_copy(got_ids, named, ls.at[1])
     load_ids.start()
     load_ids.wait()
     lane = lax.broadcasted_iota(jnp.int32, (8, LANES), 1)
@@ -241,7 +261,9 @@
 
     near_first(tiles, me, 1, drain)
     swap.wait()
-    out[...] = jnp.transpose(tot[...] + partner[...])[:PAIR]
+    full = jnp.transpose(tot[...] + partner[...])
+    for a, row in enumerate(solve_rows([full[f : f + 1, :] for f in range(27)])):
+        out[a : a + 1, :] = row
 
 
 def solve_rows(rows):
@@ -280,25 +302,26 @@
     many = pltpu.SemaphoreType.DMA((tiles,))
     pts_t, idx_t = (tiles, 3, cap, points), (tiles, cap, points)
     ids_t, sums_t = (tiles, 1, LANES), (SCANS_DEV, LANES)
-    pts, idx, ids, seg = pl.pallas_call(
-        pack_kernel,
+    block, ids, seg = pl.pallas_call(
+        plan_kernel,
         out_shape=(
-            shape(pts_t, f32),
-            shape(idx_t, i32),
+            shape((tiles * cap,), i32),
             shape(ids_t, i32),
             shape((cap // 8, tiles * 8), i32),
         ),
-        in_specs=[SMEM, SMEM, VMEM, VMEM],
-        out_specs=(VMEM, VMEM, SMEM, SMEM),
+        in_specs=[SMEM, SMEM],
+        out_specs=(SMEM, SMEM, SMEM),
         scratch_shapes=[pltpu.SMEM((tiles,), i32)],
-        name="pack",
-    )(intersection.reshape(blocks), target_scan, source_points, matches)
-    rows = pl.pallas_call(
+        name="plan",
+    )(intersection.reshape(blocks), target_scan)
+    return pl.pallas_call(
         main_kernel,
-        out_shape=shape((PAIR, SCANS_DEV), f32),
-        in_specs=[VMEM] * 6,
+        out_shape=shape((6, SCANS_DEV), f32),
+        in_specs=[SMEM] + [VMEM] * 6,
         out_specs=VMEM,
         scratch_shapes=[
+            pltpu.VMEM(pts_t, f32),
+            pltpu.VMEM(idx_t, i32),
             pltpu.VMEM(pts_t, f32),
             pltpu.VMEM(idx_t, i32),
             pltpu.VMEM(ids_t, i32),
@@ -312,11 +335,18 @@
             pltpu.VMEM(sums_t, f32),
         ]
         + [many] * 8
-        + [pltpu.SemaphoreType.DMA((4,)), pltpu.SemaphoreType.DMA, pltpu.SemaphoreType.DMA],
+        + [pltpu.SemaphoreType.DMA((2,)), pltpu.SemaphoreType.DMA, pltpu.SemaphoreType.DMA],
         compiler_params=pltpu.CompilerParams(collective_id=0, has_side_effects=True),
         name="main",
-    )(pts, idx, ids, seg, target_points, target_normals)
-    return jnp.stack(solve_rows(rows))
+    )(
+        block,
+        source_points.reshape(3, -1, 1, LANES),
+        matches.reshape(-1, 1, LANES),
+        ids,
+        seg,
+        target_points,
+        target_normals,
+    )
 
 
 def solution(mesh):

time: 56.1 us -> 52.2 us (0.930)
  local copies, waits for them, and re-layouts: 3.38 us -> 1.26 us
  other arithmetic: 1.07 us -> 0 us
  Pallas kernels: 51.3 us -> 50.7 us
    unnamed x3 -> x1, local copies, waits for them, and re-layouts: 2.77 us -> 1.26 us
    sub x3 -> x0, other arithmetic: 1.02 us -> none  [the longest x2 1 us: solve_rows(): entries[a, b] = entries[a, b] - factor * entries[k, b]]
    pallas_call x2, Pallas kernels: 51.3 us -> 50.7 us  [the longest x1 46.3 us: body(): pl.pallas_call(main_kernel, out_shape=shape((6, SCANS_DEV), f32), in_spec...]
    another operation x1 -> x0, local copies, waits for them, and re-layouts: 0.62 us -> none  [body(): return jnp.stack(solve_rows(rows))]
where the time goes in v3:
time: 52.2 us; the launch traced here: 52 us
  Pallas kernels  50.7 us (97%)
  local copies, waits for them, and re-layouts  1.26 us (2%)
    pallas_call x1, Pallas kernels, body(): pl.pallas_call(main_kernel, out_shape=shape((6, SCANS_DEV), f32), in_spec...  46.3 us
    pallas_call x1, Pallas kernels, body(): pl.pallas_call(plan_kernel, out_shape=(shape((tiles * cap,), i32), shape(...  4.33 us
    unnamed x1, local copies, waits for them, and re-layouts  1.26 us

profile of v3, /device:TPU:0, one launch (start us, length us, event | category | flops | bytes accessed | tf_op | source)
XLA Modules:
  0.0 52.0 jit_solution(16635042629176984782)
XLA Ops:
  0.0 4.3 %plan.1 = (s32[256]{0:T(256)}, s32[16,1,128]{2,1,0:T(1,128)}, s32[2,128]{1,0:T(2,128)}) custom-call(s32[128]{0:T(128)} %bitcast.5, s32[1,128]{1,0:T(1,128)} %chosen.1), custom_call_target="tpu_custom_call" | custom-call | tf_op jit(solution)/shard_map/plan/pallas_call | solution.py:305
  4.3 46.3 %main.1 = f32[6,64]{1,0:T(8,128)} custom-call(s32[256]{0:T(256)} %get-tuple-element.8.block, f32[3,256,1,128]{3,2,1,0:T(1,128)} %bitcast.3, s32[256,1,128]{2,1,0:T(1,128)} %bitcast.4, s32[16,1,128]{2,1,0:T(1,128)} %get-tuple-element.9.ids, s32[2,128]{1,0:T(2,128)} %get-tuple-element.10.seg, f32[3,32768]{1,0:T(4,128)} %tp.1, f32[3,32768]{1,0:T(4,128)} %tn.1), custom_call_target="tpu_custom_call" | custom-call | tf_op jit(solution)/shard_map/main/pallas_call | solution.py:317
  50.7 1.3 %copy.8 = f32[6,64]{1,0:T(8,128)} copy(f32[6,64]{1,0:T(8,128)} %main.1) | data formatting | bytes 3072

commit v4 on v3

--- a/solution.py
+++ b/solution.py
@@ -16,32 +16,42 @@
 SMEM = pl.BlockSpec(memory_space=pltpu.SMEM)
 
 
-def plan_kernel(dest, chosen, block, ids, seg, count):
+def plan_kernel(dest, chosen, block, ids, seg):
     tiles = ids.shape[0]
-    blocks = dest.shape[0]
-    cap = block.shape[0] // tiles
+    blocks = dest.shape[1]
+    cap = seg.shape[0] * 8
     per_scan = blocks // SCANS_DEV
-
-    def clear(t, c):
-        count[t] = 0
-        for r in range(cap):
-            block[t * cap + r] = -1
-            ids[t, 0, r] = -1
-            seg[r // 8, t * 8 + r % 8] = -1
-        return c
-
-    lax.fori_loop(0, tiles, clear, 0)
-
-    def step(b, c):
-        d = dest[b]
-        r = count[d]
-        count[d] = r + 1
-        seg[r // 8, d * 8 + r % 8] = b // per_scan
-        ids[d, 0, r] = chosen[0, b]
-        block[d * cap + r] = b
-        return c
-
-    lax.fori_loop(0, blocks, step, 0, unroll=4)
+    f32 = jnp.float32
+    hit = dest[...] == lax.broadcasted_iota(jnp.int32, (tiles, blocks), 0)
+    first = lax.broadcasted_iota(jnp.int32, (blocks, blocks), 0)
+    second = lax.broadcasted_iota(jnp.int32, (blocks, blocks), 1)
+    rank = jnp.dot(
+        hit.astype(f32), (first <= second).astype(f32), preferred_element_type=f32
+    ).astype(jnp.int32)
+    rank = jnp.where(hit, rank, 0)
+    place = lax.broadcasted_iota(jnp.int32, (tiles, blocks), 1).astype(f32) + 1.0
+    wanted = chosen[...].astype(f32) + 1.0
+    lane = lax.broadcasted_iota(jnp.int32, (tiles, LANES), 1)
+    at = jnp.zeros((tiles, LANES), f32)
+    named = jnp.zeros((tiles, LANES), f32)
+    for r in range(cap):
+        mine = rank == r + 1
+        at = jnp.where(
+            lane == r, jnp.sum(jnp.where(mine, place, 0.0), axis=1, keepdims=True), at
+        )
+        named = jnp.where(
+            lane == r, jnp.sum(jnp.where(mine, wanted, 0.0), axis=1, keepdims=True), named
+        )
+    at = at.astype(jnp.int32) - 1
+    named = named.astype(jnp.int32) - 1
+    block[...] = at
+    scan = jnp.where(at >= 0, at // per_scan, -1)
+    for t in range(tiles):
+        ids[t] = named[t : t + 1]
+    for g in range(cap // 8):
+        seg[g : g + 1, :] = jnp.concatenate(
+            [scan[t : t + 1, g * 8 : g * 8 + 8] for t in range(tiles)], axis=1
+        )
 
 
 def near_first(tiles, me, start, act):
@@ -110,7 +120,7 @@
 
     def pack(t, pts_to, idx_to):
         for r in range(cap):
-            b = block[t * cap + r]
+            b = block[t, r]
             used = jnp.minimum(b, 0) + 1
             for h in range(points // LANES):
                 span = slice(h * LANES, (h + 1) * LANES)
@@ -305,15 +315,14 @@
     block, ids, seg = pl.pallas_call(
         plan_kernel,
         out_shape=(
-            shape((tiles * cap,), i32),
+            shape((tiles, LANES), i32),
             shape(ids_t, i32),
             shape((cap // 8, tiles * 8), i32),
         ),
-        in_specs=[SMEM, SMEM],
-        out_specs=(SMEM, SMEM, SMEM),
-        scratch_shapes=[pltpu.SMEM((tiles,), i32)],
+        in_specs=[VMEM, VMEM],
+        out_specs=(VMEM, VMEM, VMEM),
         name="plan",
-    )(intersection.reshape(blocks), target_scan)
+    )(intersection.reshape(1, blocks), target_scan)
     return pl.pallas_call(
         main_kernel,
         out_shape=shape((6, SCANS_DEV), f32),

time: 52.2 us -> 49.4 us (0.946)
  Pallas kernels: 50.7 us -> 47.9 us
    pallas_call x1, Pallas kernels: 4.33 us -> 1.61 us  [body(): pl.pallas_call(plan_kernel, out_shape=(shape((tiles, LANES), i32), shape(...]
where the time goes in v4:
time: 49.4 us; the launch traced here: 49.2 us
  Pallas kernels  47.9 us (97%)
  local copies, waits for them, and re-layouts  1.27 us (3%)
    pallas_call x1, Pallas kernels, body(): pl.pallas_call(main_kernel, out_shape=shape((6, SCANS_DEV), f32), in_spec...  46.3 us
    pallas_call x1, Pallas kernels, body(): pl.pallas_call(plan_kernel, out_shape=(shape((tiles, LANES), i32), shape(...  1.61 us
    unnamed x1, local copies, waits for them, and re-layouts  1.27 us

profile of v4, /device:TPU:0, one launch (start us, length us, event | category | flops | bytes accessed | tf_op | source)
XLA Modules:
  0.0 49.2 jit_solution(6162420462927794652)
XLA Ops:
  0.0 1.6 %plan.1 = (s32[16,128]{1,0:T(8,128)}, s32[16,1,128]{2,1,0:T(1,128)}, s32[2,128]{1,0:T(2,128)}) custom-call(s32[1,128]{1,0:T(1,128)} %bitcast.5, s32[1,128]{1,0:T(1,128)} %chosen.1), custom_call_target="tpu_custom_call" | custom-call | tf_op jit(solution)/shard_map/plan/pallas_call | solution.py:315
  1.6 46.3 %main.1 = f32[6,64]{1,0:T(8,128)} custom-call(s32[16,128]{1,0:T(8,128)} %get-tuple-element.8.block, f32[3,256,1,128]{3,2,1,0:T(1,128)} %bitcast.3, s32[256,1,128]{2,1,0:T(1,128)} %bitcast.4, s32[16,1,128]{2,1,0:T(1,128)} %get-tuple-element.9.ids, s32[2,128]{1,0:T(2,128)} %get-tuple-element.10.seg, f32[3,32768]{1,0:T(4,128)} %tp.1, f32[3,32768]{1,0:T(4,128)} %tn.1), custom_call_target="tpu_custom_call" | custom-call | tf_op jit(solution)/shard_map/main/pallas_call | solution.py:326
  48.0 1.3 %copy.8 = f32[6,64]{1,0:T(8,128)} copy(f32[6,64]{1,0:T(8,128)} %main.1) | data formatting | bytes 3072
